TPU v7x, 32 devices: a whole 2x2x4 slice. The times are simulated.
32 devices in a mesh: tp: 8 (over z, y), dp: 4 (over x, core).
Axes of the slice: x: 2, y: 2, z: 4, core: 2. Of those that a mesh axis runs over, the one named last changes fastest.
Arguments:
- normed: bfloat16 [1024, 4096], P(('dp', 'tp')), may hold values from -6 to 6
- cotangent: bfloat16 [1024, 8192], P('dp', 'tp'), may hold values from -1.5 to 1.5
- weight_tiles: bfloat16 [2, 2048, 128, 128], P(None, 'tp'), may hold values from -0.09375 to 0.09375
- slot_tile: int32 [2048], replicated, may hold values from 0 to 2047, as said below
Outputs:
- hidden: bfloat16 [1024, 8192], P('dp', 'tp')
- d_normed: bfloat16 [1024, 4096], P(('dp', 'tp'))
- grad_tiles: float32 [2, 2048, 128, 128], P(None, 'tp', 'dp')
Inputs may be any that keep to these rules, and one draw needn't show every extreme that they name: `slot_tile`: A permutation of 0 to 2047. Position p belongs to owner p // 256 at slot p % 256. Each owner holds 24 to 40 tiles of the tile columns t * 8 to (t + 1) * 8 - 1 of each index t of tp; in every draw some owner holds exactly 40 for some t.
All inputs are finite; a program needn't handle non-finite values.
Results may differ from a plain program's by a relative error of at most 0.018.
Values may be sent and summed in bfloat16 or wider, within the bound.
A program may use at most 128 MiB of HBM per device.

v0:
```python
import jax
import jax.numpy as jnp
from jax import lax
from jax.sharding import PartitionSpec as P

D = 4096
FW = 8192
TILE = 128


def build_lists(slot_tile, groups, owned_count, tile_cols, cols_dev, list_len):
    owned_tiles = slot_tile.reshape(groups, owned_count)
    target = owned_tiles % tile_cols // cols_dev
    matches = (target[:, :, None] == jnp.arange(groups, dtype=jnp.int32)[None, None, :]).astype(
        jnp.int32
    )
    running = jnp.cumsum(matches, axis=1) - 1
    rank_of = jnp.sum(running * matches, axis=2)
    owner_ix = jnp.broadcast_to(jnp.arange(groups, dtype=jnp.int32)[:, None], (groups, owned_count))
    slot_ix = jnp.broadcast_to(
        jnp.arange(owned_count, dtype=jnp.int32)[None, :], (groups, owned_count)
    )
    table = jnp.full((groups, groups, list_len), -1, jnp.int32)
    return table.at[owner_ix, target, rank_of].set(slot_ix, mode="drop")


def incoming_places(in_lists, slot_tile, consumer, tile_cols, cols_dev, owned_count):
    groups = in_lists.shape[0]
    present = in_lists >= 0
    position = jnp.arange(groups, dtype=jnp.int32)[:, None] * owned_count + jnp.maximum(in_lists, 0)
    tile_id = slot_tile[position]
    tile_row = tile_id // tile_cols
    tile_col = tile_id % tile_cols - consumer * cols_dev
    local_idx = tile_row * cols_dev + tile_col
    return (jnp.where(present, local_idx, owned_count), present)


def pick_tiles(source, indices, present):
    limit = source.shape[1] - 1
    picked = source[:, jnp.minimum(indices, limit)]
    mask = present.reshape((1,) + present.shape + (1,) * (source.ndim - 2))
    return jnp.where(mask, picked, jnp.zeros((), source.dtype))


def place_tiles(arrived, places, owned_count):
    flat = arrived.reshape((arrived.shape[0], -1) + arrived.shape[3:])
    empty = jnp.zeros((arrived.shape[0], owned_count) + arrived.shape[3:], arrived.dtype)
    return empty.at[:, places.reshape(-1)].set(flat, mode="drop")


def local(normed, cotangent, weight_tiles, slot_tile):
    tp_size = lax.axis_size("tp")
    consumer = lax.axis_index("tp")
    owned_count = weight_tiles.shape[1]
    tile_size = weight_tiles.shape[2]
    tile_rows = D // TILE
    tile_cols = FW // TILE
    cols_dev = tile_cols // tp_size
    base_count = owned_count // tp_size
    list_len = base_count + base_count // 4
    send_lists = build_lists(slot_tile, tp_size, owned_count, tile_cols, cols_dev, list_len)
    my_lists = lax.dynamic_index_in_dim(send_lists, consumer, 0, keepdims=False)
    out_present = my_lists >= 0
    out_places = jnp.where(out_present, my_lists, owned_count)
    in_lists = lax.dynamic_index_in_dim(send_lists, consumer, 1, keepdims=False)
    in_places, in_present = incoming_places(
        in_lists, slot_tile, consumer, tile_cols, cols_dev, owned_count
    )
    slab_rows = tile_size // lax.axis_size("dp")
    slab_start = lax.axis_index("dp") * slab_rows
    own_rows = lax.dynamic_slice_in_dim(weight_tiles, slab_start, slab_rows, 2)
    outgoing = pick_tiles(own_rows, my_lists, out_present)
    arrived = lax.all_to_all(outgoing, "tp", split_axis=1, concat_axis=1, tiled=True)
    partial_tiles = place_tiles(arrived, in_places, owned_count)
    weight_block = lax.all_gather(partial_tiles, "dp", axis=2, tiled=True)
    weight_block = weight_block.reshape(2, tile_rows, cols_dev, tile_size, tile_size)
    gathered = lax.all_gather(normed, "tp", axis=0, tiled=True)
    group_rows = gathered.shape[0]
    tiled_in = gathered.reshape(group_rows, tile_rows, tile_size)
    both_proj = jnp.einsum(
        "nri,mrcij->nmcj", tiled_in, weight_block, preferred_element_type=jnp.float32
    )
    gate_proj = both_proj[:, 0].reshape(group_rows, -1)
    up_proj = both_proj[:, 1].reshape(group_rows, -1)
    sigmoid_gate = jax.nn.sigmoid(gate_proj)
    act_gate = gate_proj * sigmoid_gate
    hidden = (act_gate * up_proj).astype(jnp.bfloat16)
    cot_full = cotangent.astype(jnp.float32)
    grad_gate = (
        cot_full * up_proj * (sigmoid_gate * (1.0 + gate_proj * (1.0 - sigmoid_gate)))
    ).astype(jnp.bfloat16)
    grad_up = (cot_full * act_gate).astype(jnp.bfloat16)
    grads_in = jnp.stack([grad_gate, grad_up], 1).reshape(group_rows, 2, cols_dev, tile_size)
    term = jnp.einsum("nmcj,mrcij->nri", grads_in, weight_block, preferred_element_type=jnp.float32)
    d_normed = lax.psum_scatter(
        term.reshape(normed.shape[0] * lax.axis_size("tp"), -1).astype(jnp.bfloat16),
        "tp",
        scatter_dimension=0,
        tiled=True,
    )
    partial_value = jnp.einsum(
        "nri,nmcj->mrcij", tiled_in, grads_in, preferred_element_type=jnp.float32
    ).astype(jnp.bfloat16)
    partial_value = partial_value.reshape(2, owned_count, tile_size, tile_size)
    summed = lax.psum_scatter(partial_value, "dp", scatter_dimension=2, tiled=True).astype(
        jnp.float32
    )
    outgoing_grads = pick_tiles(summed, in_places, in_present)
    returned = lax.all_to_all(
        outgoing_grads.astype(jnp.bfloat16), "tp", split_axis=1, concat_axis=1, tiled=True
    ).astype(outgoing_grads.dtype)
    result = place_tiles(returned, out_places, owned_count)
    return (hidden, d_normed, result)


def solution(mesh):
    return jax.shard_map(
        local,
        mesh=mesh,
        in_specs=(P(("dp", "tp"), None), P("dp", "tp"), P(None, "tp", None, None), P()),
        out_specs=(P("dp", "tp"), P(("dp", "tp"), None), P(None, "tp", "dp", None)),
        check_vma=False,
    )
```

profile of v0, /device:TPU:0, one launch (start us, length us, event | category | flops | bytes accessed | tf_op | source)
XLA Modules:
  0.0 721.2 jit_solution(2535239984476430002)
XLA Ops:
  7.2 0.7 reshape.556
  7.9 0.7 reshape.555
  8.6 0.7 and_select_fusion
  9.3 4.5 reduce-window.6
  13.9 0.2 copy.31
  14.2 0.1 fusion.20
  14.3 0.7 and_reduce_fusion
  15.1 0.7 multiply_reduce_fusion
  15.8 8.1 %scatter_custom_fusion.2 = s32[2560]{0:T(1024)S(1)} fusion(s32[2048]{0:T(1024)S(1)} %bitcast.129, s32[2048]{0:T(1024)S(1)} %bitcast.130, s32[]{:T(128)} %constant.86.clone.1), kind=kCustom, calls=%fused_computation.84 | custom fusion | bytes 10244
  23.9 0.1 reshape.568
  24.0 0.1 reshape.581
  24.1 4.9 constant_dynamic-slice_fusion
  29.0 5.9 gather_fusion.1
  34.9 5.3 select_bitcast_fusion
  40.2 7.4 %all-to-all-start = ((bf16[2,8,40,32,128]{4,3,0,2,1:T(8,128)(2,1)}), bf16[2,8,40,32,128]{4,3,0,2,1:T(8,128)(2,1)}, u32[]{:S(2)}, u32[]{:S(2)}) async-start(bf16[2,8,40,32,128]{4,3,0,2,1:T(8,128)(2,1)} %select_bitcast_fusion), calls=%async_computation | async-start | bytes 10485760 | tf_op jit(solution)/shard_map/all_to_all | solution.py:73
  47.7 0.7 all-gather.5.cloned.1.call-update
  48.5 0.1 reshape.573
  48.6 2.2 gather_fusion
  50.9 0.1 gather.16
  51.0 0.1 ge.52
  51.1 137.6 %all-to-all-done = bf16[2,8,40,32,128]{4,3,0,2,1:T(8,128)(2,1)} async-done(((bf16[2,8,40,32,128]{4,3,0,2,1:T(8,128)(2,1)}), bf16[2,8,40,32,128]{4,3,0,2,1:T(8,128)(2,1)}, u32[]{:S(2)}, u32[]{:S(2)}) %all-to-all-start) | async-done | bytes 5242912 | tf_op jit(solution)/shard_map/all_to_all | solution.py:73
  188.7 2.6 broadcast_in_dim.63
  191.3 43.5 %scatter_fusion = bf16[2,256,32,128]{3,2,1,0:T(8,128)(2,1)} fusion(bf16[2,256,32,128]{3,2,1,0:T(8,128)(2,1)} %broadcast_in_dim.63, s32[320]{0:T(512)S(1)} %fusion.42, bf16[320,2,32,128]{3,2,1,0:T(8,128)(2,1)} %bitcast.13), kind=kCustom, calls=%fused_computation.3 | custom fusion | bytes 15729920 | tf_op jit(solution)/shard_map/scatter | solution.py:48
  234.8 0.2 reduce-scatter.5.cloned.1.call-start
  235.0 0.2 copy.38
  235.3 3.3 copy.35
  238.6 100.3 %all-gather.3.cloned.1.call-done = bf16[2,256,128,128]{3,2,1,0:T(8,128)(2,1)} async-done(((bf16[2,256,32,128]{3,2,1,0:T(8,128)(2,1)}), bf16[2,256,128,128]{3,2,1,0:T(8,128)(2,1)}) %all-gather.3.cloned.1.call-update) | async-done | bytes 16777232 | tf_op jit(solution)/shard_map/all_gather | solution.py:75
  338.9 8.1 %convolution_bitcast_fusion = f32[256,2,8,128]{0,3,2,1:T(8,128)S(1)} fusion(bf16[2,32,8,128,128]{4,3,2,1,0:T(8,128)(2,1)} %bitcast.115, bf16[256,32,128,1,1]{0,2,4,1,3:T(8,128)(2,1)S(1)} %bitcast.120), kind=kOutput, calls=%fused_computation.15 | convolution fusion | flops 4294967296 | bytes 20971520 | tf_op jit(solution)/shard_map/nri,mrcij->nmcj/dot_general | solution.py:80
  347.0 0.2 fusion.49
  347.2 1.6 fusion.10
  348.9 0.3 copy.40
  349.1 1.3 copy.39
  350.5 8.1 %convert_bitcast_fusion = bf16[2,32,8,128,128]{3,4,1,2,0:T(8,128)(2,1)} fusion(bf16[256,32,128,1,1]{0,2,1,4,3:T(8,128)(2,1)S(1)} %bitcast.121, bf16[256,1,8,128]{3,0,1,2:T(8,128)(2,1)S(1)} %copy.40, bf16[256,1,8,128]{3,0,1,2:T(8,128)(2,1)S(1)} %copy.39), kind=kOutput, calls=%fused_computation.8 | convolution fusion | flops 4303880192 | bytes 19922944 | tf_op jit(solution)/shard_map/nri,nmcj->mrcij/dot_general | solution.py:101
  358.6 21.2 %copy.45 = bf16[2,32,8,128,128]{4,3,2,1,0:T(8,128)(2,1)} copy(bf16[2,32,8,128,128]{3,4,1,2,0:T(8,128)(2,1)} %convert_bitcast_fusion) | data formatting | bytes 33554432 | tf_op jit(solution)/shard_map/convert_element_type | solution.py:103
  379.8 0.1 reshape.589
  379.9 124.9 %reduce-scatter.5.cloned.1.call-done = bf16[2,256,32,128]{3,2,1,0:T(8,128)(2,1)} async-done(((bf16[2,256,128,128]{3,2,1,0:T(8,128)(2,1)}), bf16[2,256,32,128]{3,2,1,0:T(8,128)(2,1)}) %reduce-scatter.5.cloned.1.call-update) | async-done | bytes 4194320 | tf_op jit(solution)/shard_map/reduce_scatter | solution.py:105
  504.8 5.9 gather_fusion.2
  510.7 6.0 fusion.5
  516.7 5.5 all-to-all-start.1
  522.3 0.3 reduce-scatter.3.cloned.1.call-start
  522.5 18.6 %copy.41 = bf16[32,128,8,128,2]{3,2,4,1,0:T(8,128)(2,1)} copy(bf16[32,128,8,128,2]{3,1,2,0,4:T(8,128)(2,1)} %bitcast.116) | data formatting | bytes 33554432 | tf_op jit(solution)/shard_map/nmcj,mrcij->nri/dot_general | solution.py:94
  541.1 12.6 %fusion.6 = bf16[256,4096]{1,0:T(8,128)(2,1)} fusion(bf16[4096,8,128,2]{2,1,3,0:T(8,128)(2,1)} %bitcast.122, bf16[256,1,8,128]{3,0,1,2:T(8,128)(2,1)S(1)} %copy.40, bf16[256,1,8,128]{3,0,1,2:T(8,128)(2,1)S(1)} %copy.39), kind=kOutput, calls=%fused_computation.14 | convolution fusion | flops 4296540160 | bytes 19922944 | tf_op jit(solution)/shard_map/nmcj,mrcij->nri/dot_general | solution.py:94
  553.7 0.1 squeeze.6
  553.8 1.0 copy.46
  554.8 99.9 %all-to-all-done.1 = bf16[2,8,40,32,128]{4,3,0,2,1:T(8,128)(2,1)} async-done(((bf16[2,8,40,32,128]{4,3,0,2,1:T(8,128)(2,1)}), bf16[2,8,40,32,128]{4,3,0,2,1:T(8,128)(2,1)}, u32[]{:S(2)}, u32[]{:S(2)}) %all-to-all-start.1) | async-done | bytes 5242912 | tf_op jit(solution)/shard_map/all_to_all | solution.py:109
  654.7 8.0 %convert_bitcast_fusion.1 = f32[320,2,32,128]{3,2,1,0:T(8,128)} fusion(bf16[2,8,40,32,128]{4,3,0,2,1:T(8,128)(2,1)} %all-to-all-done.1), kind=kLoop, calls=%fused_computation.9 | loop fusion | flops 2621440 | bytes 15728640 | tf_op jit(solution)/shard_map/reshape | solution.py:46
  662.6 4.5 broadcast_in_dim.71
  667.1 47.5 %scatter_fusion.1 = f32[2,256,32,128]{3,2,1,0:T(8,128)} fusion(f32[2,256,32,128]{3,2,1,0:T(8,128)} %broadcast_in_dim.71, s32[320]{0:T(512)S(1)} %fusion.43, f32[320,2,32,128]{3,2,1,0:T(8,128)} %convert_bitcast_fusion.1), kind=kCustom, calls=%fused_computation.4 | custom fusion | bytes 31458560 | tf_op jit(solution)/shard_map/scatter | solution.py:48
  (37 shorter events, 0.6 us)
Async XLA Ops:
  40.2 8.4 %copy-start = (s32[2048]{0:T(1024)S(1)}, s32[2048]{0:T(1024)}, u32[]{:S(2)}) copy-start(s32[2048]{0:T(1024)} %param.7) | copy-start | bytes 24580
  40.2 148.5 %all-to-all-start = ((bf16[2,8,40,32,128]{4,3,0,2,1:T(8,128)(2,1)}), bf16[2,8,40,32,128]{4,3,0,2,1:T(8,128)(2,1)}, u32[]{:S(2)}, u32[]{:S(2)}) async-start(bf16[2,8,40,32,128]{4,3,0,2,1:T(8,128)(2,1)} %select_bitcast_fusion), calls=%async_computation | async-start | bytes 10485760 | tf_op jit(solution)/shard_map/all_to_all | solution.py:73
  47.6 187.6 %all-gather.5.cloned.1.call-start = ((), (), s32[]{:S(2)}) async-start(), calls=%async_computation.5 | async-start | bytes 2359296 | tf_op jit(solution)/shard_map/all_gather | solution.py:77
  48.4 290.5 %all-gather.3.cloned.1.call-start = ((), (), s32[]{:S(2)}) async-start(), calls=%async_computation.4 | async-start | bytes 20971520 | tf_op jit(solution)/shard_map/all_gather | solution.py:75
  191.3 43.8 %copy-start.2 = (bf16[256,1024]{1,0:T(8,128)(2,1)S(1)}, bf16[256,1024]{1,0:T(8,128)(2,1)}, u32[]{:S(2)}) copy-start(bf16[256,1024]{1,0:T(8,128)(2,1)} %param.5) | copy-start | bytes 1572868
  234.8 270.0 %reduce-scatter.5.cloned.1.call-start = ((), (), s32[]{:S(2)}) async-start(), calls=%async_computation.7 | async-start | bytes 20971520 | tf_op jit(solution)/shard_map/reduce_scatter | solution.py:105
  516.7 137.9 %all-to-all-start.1 = ((bf16[2,8,40,32,128]{4,3,0,2,1:T(8,128)(2,1)}), bf16[2,8,40,32,128]{4,3,0,2,1:T(8,128)(2,1)}, u32[]{:S(2)}, u32[]{:S(2)}) async-start(bf16[2,8,40,32,128]{4,3,0,2,1:T(8,128)(2,1)} %fusion.5), calls=%async_computation.3 | async-start | bytes 10485760 | tf_op jit(solution)/shard_map/all_to_all | solution.py:109
  522.3 192.4 %reduce-scatter.3.cloned.1.call-start = ((), (), s32[]{:S(2)}) async-start(), calls=%async_computation.6 | async-start | bytes 2359296 | tf_op jit(solution)/shard_map/reduce_scatter | solution.py:95
  541.1 12.7 %copy-start.1 = (bf16[256,1024]{0,1:T(8,128)(2,1)S(1)}, bf16[256,1024]{0,1:T(8,128)(2,1)}, u32[]{:S(2)}) copy-start(bf16[256,1024]{0,1:T(8,128)(2,1)} %get-tuple-element.16) | copy-start | bytes 1572868
Sparse Core Ops, SparseCore 0:
  50.6 119.8 all-gather.4
  234.9 103.8 all-gather.2
  379.9 124.8 reduce-scatter.4
  553.8 121.1 reduce-scatter.2
where the time goes:
time: 724 us; the launch traced here: 721 us
  waiting for transfers between devices  463 us (64%)
  local copies, waits for them, and re-layouts  173 us (24%)
  matrix products  28.8 us (4%)
  other arithmetic  28 us (4%)
  between operations  14 us (2%)
  starting transfers between devices  13.5 us (2%)
    all_to_all x1, waiting for transfers between devices, local(): lax.all_to_all(outgoing, 'tp', split_axis=1, concat_axis=1, tiled=True)  138 us
    reduce_scatter x1, waiting for transfers between devices, local(): lax.psum_scatter(partial_value, 'dp', scatter_dimension=2, tiled=True)  125 us
    all_gather x1, waiting for transfers between devices, local(): weight_block = lax.all_gather(partial_tiles, 'dp', axis=2, tiled=True)  100 us
    all_to_all x1, waiting for transfers between devices, local(): lax.all_to_all(outgoing_grads.astype(jnp.bfloat16), 'tp', split_axis=1, c...  99.9 us
    scatter x2, local copies, waits for them, and re-layouts, place_tiles(): return empty.at[:, places.reshape(-1)].set(flat, mode='drop')  91 us
    convert_element_type x1, local copies, waits for them, and re-layouts, local(): partial_value = jnp.einsum('nri,nmcj->mrcij', tiled_in, grads_in, preferr...  21.2 us
    dot_general x1, local copies, waits for them, and re-layouts, local(): jnp.einsum('nmcj,mrcij->nri', grads_in, weight_block, preferred_element_t...  18.6 us
  transfers between devices with their start and end apart: 6, of which 4 were waited for; matrix products, arithmetic and copies ran while one was open for 20% of the time, Pallas kernels for 0%

commit v1 on v0

v1 whole, which is shorter than its diff:
```python
import jax
import jax.numpy as jnp
from jax import lax
from jax.experimental import pallas as pl
from jax.experimental.pallas import tpu as pltpu
from jax.sharding import PartitionSpec as P


def index_tables(slot_tile, groups, me, owned_count, tile_rows, tile_cols, list_len):
    cols_dev = tile_cols // groups
    tiles = slot_tile.reshape(groups, owned_count)
    target = tiles % tile_cols // cols_dev
    before = jnp.arange(owned_count)[:, None] < jnp.arange(owned_count)[None, :]
    ranks = jnp.arange(list_len, dtype=jnp.int32)
    devices = jnp.arange(groups, dtype=jnp.int32)
    my_target = lax.dynamic_index_in_dim(target, me, 0, keepdims=False)
    same = (my_target[:, None] == my_target[None, :]) & before
    my_rank = jnp.sum(same.astype(jnp.int32), axis=0)
    my_key = my_target * list_len + my_rank
    keys = (devices[:, None] * list_len + ranks[None, :]).reshape(-1)
    slots = jnp.arange(owned_count, dtype=jnp.int32)
    send_slots = jnp.sum(jnp.where(keys[:, None] == my_key[None, :], slots[None, :], 0), axis=1)
    mine = target == me
    rank = jnp.dot(
        mine.astype(jnp.bfloat16), before.astype(jnp.bfloat16), preferred_element_type=jnp.float32
    ).astype(jnp.int32)
    place = devices[:, None] * list_len + rank
    local_ix = (tiles % tile_cols - me * cols_dev) * tile_rows + tiles // tile_cols
    local_ix = jnp.where(mine, local_ix, -1)
    flat_local = local_ix.reshape(-1)
    blocks = jnp.arange(owned_count, dtype=jnp.int32)
    from_place = jnp.sum(
        jnp.where(blocks[:, None] == flat_local[None, :], place.reshape(-1)[None, :], 0), axis=1
    )
    hit = mine[:, None, :] & (rank[:, None, :] == ranks[None, :, None])
    return_ix = jnp.sum(jnp.where(hit, local_ix[:, None, :], 0), axis=2).reshape(-1)
    return send_slots, my_key, from_place, return_ix


def take_tiles(source, indices):
    flat = source.reshape((-1,) + source.shape[-2:])
    return jnp.take(flat, indices.reshape(-1), axis=0, mode="clip")


def project_kernel(banded_ref, weights_ref, out_ref):
    pair = jnp.concatenate([weights_ref[0], weights_ref[1]], axis=1)
    out_ref[...] = jnp.dot(
        banded_ref[...], pair, preferred_element_type=jnp.float32
    ).astype(out_ref.dtype)


def project(banded, weights):
    tokens, depth = banded.shape
    blocks, _, tile = weights.shape
    chunk = min(tokens, 1024)
    return pl.pallas_call(
        project_kernel,
        grid=(tokens // chunk, blocks // 2),
        in_specs=[
            pl.BlockSpec((chunk, depth), lambda n, b: (n, 0)),
            pl.BlockSpec((2, depth, tile), lambda n, b: (b, 0, 0)),
        ],
        out_specs=pl.BlockSpec((chunk, 2 * tile), lambda n, b: (n, b)),
        out_shape=jax.ShapeDtypeStruct((tokens, blocks * tile), jnp.bfloat16),
        cost_estimate=pl.CostEstimate(
            flops=2 * tokens * depth * blocks * tile,
            bytes_accessed=2 * (tokens * depth + depth * blocks * tile + tokens * blocks * tile),
            transcendentals=0,
        ),
    )(banded, weights)


def outer_kernel(banded_t_ref, grads_ref, out_ref, total_ref):
    step = pl.program_id(1)
    tile = out_ref.shape[2]
    term = jnp.dot(banded_t_ref[...], grads_ref[...], preferred_element_type=jnp.float32)

    @pl.when(step == 0)
    def _():
        total_ref[...] = term

    @pl.when(step > 0)
    def _():
        total_ref[...] += term

    @pl.when(step == pl.num_programs(1) - 1)
    def _():
        for half in range(2):
            part = total_ref[:, half * tile : (half + 1) * tile]
            out_ref[half] = part.astype(out_ref.dtype)


def outer(banded_t, grads, tile):
    depth, tokens = banded_t.shape
    blocks = grads.shape[1] // tile
    chunk = min(tokens, 1024)
    return pl.pallas_call(
        outer_kernel,
        grid=(blocks // 2, tokens // chunk),
        in_specs=[
            pl.BlockSpec((depth, chunk), lambda b, n: (0, n)),
            pl.BlockSpec((chunk, 2 * tile), lambda b, n: (n, b)),
        ],
        out_specs=pl.BlockSpec((2, depth, tile), lambda b, n: (b, 0, 0)),
        out_shape=jax.ShapeDtypeStruct((blocks, depth, tile), jnp.bfloat16),
        scratch_shapes=[pltpu.VMEM((depth, 2 * tile), jnp.float32)],
        cost_estimate=pl.CostEstimate(
            flops=2 * tokens * depth * blocks * tile,
            bytes_accessed=2 * (tokens * depth + depth * blocks * tile + tokens * blocks * tile),
            transcendentals=0,
        ),
    )(banded_t, grads)


def local(normed, cotangent, weight_tiles, slot_tile):
    tp_size = lax.axis_size("tp")
    dp_size = lax.axis_size("dp")
    me_tp = lax.axis_index("tp")
    me_dp = lax.axis_index("dp")
    rows, width = normed.shape
    group_rows, cols = cotangent.shape
    owned_count, tile = weight_tiles.shape[1:3]
    tile_rows = width // tile
    cols_dev = cols // tile
    tile_cols = cols_dev * tp_size
    base_count = owned_count // tp_size
    list_len = base_count + base_count // 4
    band = tile // dp_size
    depth = tile_rows * band
    tokens = group_rows * dp_size
    send_slots, my_key, from_place, return_ix = index_tables(
        slot_tile, tp_size, me_tp, owned_count, tile_rows, tile_cols, list_len
    )

    by_band = normed.reshape(rows, tile_rows, dp_size, band).transpose(2, 0, 1, 3)
    by_band = by_band.reshape(dp_size, rows, depth)
    by_group = lax.all_to_all(by_band, "dp", split_axis=0, concat_axis=0, tiled=True)
    banded = lax.all_gather(by_group, "tp", axis=1, tiled=True).reshape(tokens, depth)

    both = jnp.arange(2, dtype=jnp.int32)
    send_ix = send_slots.reshape(tp_size, 1, list_len) + both[None, :, None] * owned_count
    in_ix = (from_place // list_len * 2 + both[:, None]) * list_len + from_place % list_len
    back_ix = return_ix.reshape(tp_size, 1, list_len) + both[None, :, None] * owned_count
    out_ix = (my_key // list_len * 2 + both[:, None]) * list_len + my_key % list_len
    travel = (tp_size, 2 * list_len, band, tile)
    own_rows = lax.dynamic_slice_in_dim(weight_tiles, me_dp * band, band, 2)
    outgoing = take_tiles(own_rows, send_ix).reshape(travel)
    arrived = lax.all_to_all(outgoing, "tp", split_axis=0, concat_axis=0, tiled=True)
    weights = take_tiles(arrived, in_ix).reshape(2 * cols_dev, depth, tile)

    partial = project(banded, weights)
    proj = lax.psum_scatter(partial, "dp", scatter_dimension=0, tiled=True).astype(jnp.float32)
    gate_proj = proj[:, :cols]
    up_proj = proj[:, cols:]
    sigmoid_gate = jax.nn.sigmoid(gate_proj)
    act_gate = gate_proj * sigmoid_gate
    hidden = (act_gate * up_proj).astype(jnp.bfloat16)
    cot_full = cotangent.astype(jnp.float32)
    grad_gate = (
        cot_full * up_proj * (sigmoid_gate * (1.0 + gate_proj * (1.0 - sigmoid_gate)))
    ).astype(jnp.bfloat16)
    grad_up = (cot_full * act_gate).astype(jnp.bfloat16)
    grads = jnp.concatenate([grad_gate, grad_up], axis=1)
    grads = lax.all_gather(grads, "dp", axis=0, tiled=True)

    summed = outer(banded.T, grads, tile).reshape(2 * owned_count, band, tile)
    back = take_tiles(summed, back_ix).reshape(travel)
    back, grads = lax.optimization_barrier((back, grads))
    returned = lax.all_to_all(back, "tp", split_axis=0, concat_axis=0, tiled=True)
    result = take_tiles(returned, out_ix).astype(jnp.float32)
    result = result.reshape(2, owned_count, band, tile)

    grads = grads.reshape(tokens, 2 * cols_dev, tile)
    term = jnp.einsum("nbj,bkj->nk", grads, weights, preferred_element_type=jnp.float32)
    term = term.astype(jnp.bfloat16).reshape(dp_size, tp_size, rows, depth).transpose(1, 0, 2, 3)
    d_band = lax.psum_scatter(term.reshape(-1, depth), "tp", scatter_dimension=0, tiled=True)
    d_band = d_band.reshape(dp_size, rows, depth)
    d_rows = lax.all_to_all(d_band, "dp", split_axis=0, concat_axis=0, tiled=True)
    d_normed = d_rows.reshape(dp_size, rows, tile_rows, band).transpose(1, 2, 0, 3)
    return (hidden, d_normed.reshape(rows, width), result)


def solution(mesh):
    return jax.shard_map(
        local,
        mesh=mesh,
        in_specs=(P(("dp", "tp"), None), P("dp", "tp"), P(None, "tp", None, None), P()),
        out_specs=(P("dp", "tp"), P(("dp", "tp"), None), P(None, "tp", "dp", None)),
        check_vma=False,
    )
```

time: 724 us -> 519 us (0.72)
  local copies, waits for them, and re-layouts: 173 us -> 50.3 us
  waiting for transfers between devices: 463 us -> 389 us
  matrix products: 28.8 us -> 8.13 us
  Pallas kernels: 0 us -> 20 us
  other arithmetic: 28 us -> 12.1 us
  blocking collectives: 0 us -> 9.38 us
    all_to_all x2 -> x3, waiting for transfers between devices: 237 us -> 120 us  [the longest x1 112 us: local(): lax.all_to_all(back, 'tp', split_axis=0, concat_axis=0, tiled=True)]
    scatter x3 -> x0, local copies, waits for them, and re-layouts: 91.1 us -> none  [the longest x2 91 us: place_tiles(): return empty.at[:, places.reshape(-1)].set(flat, mode='drop')]
    all_gather x2, waiting for transfers between devices: 100 us -> 156 us  [the longest x1 122 us: local(): lax.all_gather(by_group, 'tp', axis=1, tiled=True).reshape(tokens, depth)]
    convert_element_type x1 -> x0, local copies, waits for them, and re-layouts: 21.2 us -> none  [local(): partial_value = jnp.einsum('nri,nmcj->mrcij', tiled_in, grads_in, preferr...]
    dot_general x3 -> x2, matrix products: 28.8 us -> 8.13 us  [the longest x1 7.98 us: local(): jnp.einsum('nbj,bkj->nk', grads, weights, preferred_element_type=jnp.floa...]
    pallas_call x0 -> x2, Pallas kernels: none -> 20 us  [the longest x1 9.98 us: project(): pl.pallas_call(project_kernel, grid=(tokens // chunk, blocks // 2), in_sp...]
    dot_general x1 -> x0, local copies, waits for them, and re-layouts: 18.6 us -> none  [local(): jnp.einsum('nmcj,mrcij->nri', grads_in, weight_block, preferred_element_t...]
    reduce_scatter x2, waiting for transfers between devices: 125 us -> 112 us  [the longest x1 68.6 us: local(): lax.psum_scatter(term.reshape(-1, depth), 'tp', scatter_dimension=0, tile...]
  transfers between devices with their start and end apart: 6 -> 7, of which waited for: 4 -> 6; matrix products, arithmetic and copies ran while one was open for 20% -> 5% of each run, Pallas kernels for 0% -> 0%
where the time goes in v1:
time: 519 us; the launch traced here: 518 us
  waiting for transfers between devices  389 us (75%)
  local copies, waits for them, and re-layouts  50.3 us (10%)
  Pallas kernels  20 us (4%)
  starting transfers between devices  15.7 us (3%)
  between operations  14 us (3%)
  other arithmetic  12.1 us (2%)
  blocking collectives  9.38 us (2%)
  matrix products  8.13 us (2%)
    all_gather x1, waiting for transfers between devices, local(): lax.all_gather(by_group, 'tp', axis=1, tiled=True).reshape(tokens, depth)  122 us
    all_to_all x1, waiting for transfers between devices, local(): lax.all_to_all(back, 'tp', split_axis=0, concat_axis=0, tiled=True)  112 us
    reduce_scatter x1, waiting for transfers between devices, local(): lax.psum_scatter(term.reshape(-1, depth), 'tp', scatter_dimension=0, tile...  68.6 us
    reduce_scatter x1, waiting for transfers between devices, local(): lax.psum_scatter(partial, 'dp', scatter_dimension=0, tiled=True)  43.8 us
    all_gather x1, waiting for transfers between devices, local(): grads = lax.all_gather(grads, 'dp', axis=0, tiled=True)  34.3 us
    gather x4, local copies, waits for them, and re-layouts, take_tiles(): return jnp.take(flat, indices.reshape(-1), axis=0, mode='clip')  25.1 us
  transfers between devices with their start and end apart: 7, of which 6 were waited for; matrix products, arithmetic and copies ran while one was open for 5% of the time, Pallas kernels for 0%

profile of v1, /device:TPU:0, one launch (start us, length us, event | category | flops | bytes accessed | tf_op | source)
XLA Modules:
  0.0 518.2 jit_solution(4345141220213577163)
XLA Ops:
  7.2 1.7 reshape.367
  8.9 0.2 copy.45
  9.1 1.8 reshape.368
  10.9 4.2 all-to-all-start
  15.2 0.1 convolution_convert_fusion
  15.3 0.1 convert_reduce_fusion
  15.5 0.1 iota_add_fusion
  15.6 0.1 add.254
  15.6 0.2 select_reduce_fusion.2
  15.9 0.1 add.258
  15.9 0.2 select_reduce_fusion.1
  16.2 0.1 broadcast_add_fusion
  16.3 0.1 reshape.387
  16.4 4.9 constant_dynamic-slice_fusion.1
  21.3 6.9 %gather_fusion = bf16[640,32,128]{2,1,0:T(8,128)(2,1)} fusion(bf16[512,32,128]{2,1,0:T(8,128)(2,1)} %bitcast.53, s32[1024]{0:T(1024)S(1)} %pad_clamp_fusion.3), kind=kCustom, calls=%fused_computation | custom fusion | bytes 10488320 | tf_op jit(solution)/shard_map/jit(_take)/gather | solution.py:42
  28.1 6.5 %all-to-all-start.1 = ((bf16[8,80,32,128]{3,2,1,0:T(8,128)(2,1)}), bf16[8,80,32,128]{3,2,1,0:T(8,128)(2,1)}, u32[]{:S(2)}, u32[]{:S(2)}) async-start(bf16[8,80,32,128]{3,2,1,0:T(8,128)(2,1)} %bitcast.54), calls=%async_computation.1 | async-start | bytes 10485760 | tf_op jit(solution)/shard_map/all_to_all | solution.py:148
  34.7 0.9 copy.27
  35.6 0.0 reduce-scatter.3.cloned.1.call-start
  35.7 0.1 add_bitcast_fusion
  35.8 0.3 select_reduce_fusion
  36.1 121.9 %all-gather.3.cloned.1.call-done = bf16[4,256,1024]{2,0,1:T(4,128)(2,1)} async-done(((bf16[4,32,1024]{2,0,1:T(4,128)(2,1)}), bf16[4,256,1024]{2,0,1:T(4,128)(2,1)}) %all-gather.3.cloned.1.call-update) | async-done | bytes 2097168 | tf_op jit(solution)/shard_map/all_gather | solution.py:138
  158.1 5.7 %copy.28 = bf16[4,256,1024]{1,0,2:T(4,128)(2,1)} copy(bf16[4,256,1024]{2,0,1:T(4,128)(2,1)} %all-gather.3.cloned.1.call-done) | data formatting | bytes 4194304 | tf_op jit(solution)/shard_map/all_gather | solution.py:138
  163.7 2.1 copy.34
  165.8 2.6 copy.29.banded_ref
  168.4 7.9 %all-to-all-done.1 = bf16[8,80,32,128]{3,2,1,0:T(8,128)(2,1)} async-done(((bf16[8,80,32,128]{3,2,1,0:T(8,128)(2,1)}), bf16[8,80,32,128]{3,2,1,0:T(8,128)(2,1)}, u32[]{:S(2)}, u32[]{:S(2)}) %all-to-all-start.1) | async-done | bytes 5242912 | tf_op jit(solution)/shard_map/all_to_all | solution.py:148
  176.3 5.6 %gather_fusion.1 = bf16[512,32,128]{2,1,0:T(8,128)(2,1)} fusion(bf16[640,32,128]{2,1,0:T(8,128)(2,1)} %bitcast.6, s32[1024]{0:T(1024)S(1)} %pad_clamp_fusion.2), kind=kCustom, calls=%fused_computation.1 | custom fusion | bytes 8390656 | tf_op jit(solution)/shard_map/jit(_take)/gather | solution.py:42
  182.0 10.0 %shard_map.67 = bf16[1024,2048]{1,0:T(8,128)(2,1)} custom-call(bf16[1024,1024]{1,0:T(8,128)(2,1)} %copy.29.banded_ref, bf16[16,1024,128]{2,1,0:T(8,128)(2,1)} %bitcast.62), custom_call_target="tpu_custom_call" | custom-call | flops 4294967296 | bytes 10485760 | tf_op jit(solution)/shard_map/pallas_call | solution.py:56
  192.0 0.0 all-gather.5.cloned.1.call-start
  192.0 43.8 %reduce-scatter.3.cloned.1.call-done = bf16[256,2048]{1,0:T(8,128)(2,1)} async-done(((bf16[1024,2048]{1,0:T(8,128)(2,1)}), bf16[256,2048]{1,0:T(8,128)(2,1)}) %reduce-scatter.3.cloned.1.call-update) | async-done | bytes 1048592 | tf_op jit(solution)/shard_map/reduce_scatter | solution.py:152
  235.8 1.5 convert_element_type.35
  237.3 1.6 fusion.6
  238.9 1.1 pad_maximum_fusion
  240.0 0.2 reduce-scatter.5.cloned.1.call-start
  240.2 0.1 reshape.403
  240.3 34.3 %all-gather.5.cloned.1.call-done.grads_ref = bf16[1024,2048]{1,0:T(8,128)(2,1)} async-done(((bf16[256,2048]{1,0:T(8,128)(2,1)}), bf16[1024,2048]{1,0:T(8,128)(2,1)}) %all-gather.5.cloned.1.call-update) | async-done | bytes 4194320 | tf_op jit(solution)/shard_map/all_gather | solution.py:164
  274.6 10.0 %shard_map.68 = bf16[16,1024,128]{2,1,0:T(8,128)(2,1)} custom-call(bf16[1024,1024]{1,0:T(8,128)(2,1)} %bitcast.58, bf16[1024,2048]{1,0:T(8,128)(2,1)} %all-gather.5.cloned.1.call-done.grads_ref), custom_call_target="tpu_custom_call" | custom-call | flops 4294967296 | bytes 10485760 | tf_op jit(solution)/shard_map/pallas_call | solution.py:97
  284.6 6.9 %gather_fusion.2 = bf16[640,32,128]{2,1,0:T(8,128)(2,1)} fusion(bf16[512,32,128]{2,1,0:T(8,128)(2,1)} %bitcast.61, s32[1024]{0:T(1024)S(1)} %pad_clamp_fusion.1), kind=kCustom, calls=%fused_computation.2 | custom fusion | bytes 10488320 | tf_op jit(solution)/shard_map/jit(_take)/gather | solution.py:42
  291.5 8.0 %bitcast_convert_fusion = bf16[1024,1024]{1,0:T(8,128)(2,1)S(1)} fusion(bf16[16,1024,128]{2,1,0:T(8,128)(2,1)} %bitcast.63, bf16[1024,2048]{1,0:T(8,128)(2,1)} %all-gather.5.cloned.1.call-done.grads_ref), kind=kOutput, calls=%fused_computation.7 | convolution fusion | flops 4296015872 | bytes 10485760 | tf_op jit(solution)/shard_map/nbj,bkj->nk/dot_general | solution.py:174
  299.4 1.5 copy.31
  301.0 68.6 %reduce-scatter.5.cloned.1.call-done = bf16[128,1024]{1,0:T(8,128)(2,1)} async-done(((bf16[1024,1024]{1,0:T(8,128)(2,1)}), bf16[128,1024]{1,0:T(8,128)(2,1)}) %reduce-scatter.5.cloned.1.call-update) | async-done | bytes 262160 | tf_op jit(solution)/shard_map/reduce_scatter | solution.py:176
  369.6 9.4 %all_to_all.20 = bf16[4,32,1024]{2,1,0:T(8,128)(2,1)S(1)} all-to-all(bf16[4,32,1024]{2,1,0:T(8,128)(2,1)} %bitcast.67), channel_id=1, replica_groups=mesh['tp'=8,'dp'=4] {'dp'}, dimensions={0} | all-to-all | bytes 524288 | tf_op jit(solution)/shard_map/all_to_all | solution.py:178
  378.9 4.6 all-to-all-start.3
  383.6 0.8 reshape.381
  384.4 0.8 copy.32
  385.2 1.8 reshape.382
  387.1 112.1 %all-to-all-done.3 = bf16[8,80,32,128]{3,2,1,0:T(8,128)(2,1)} async-done(((bf16[8,80,32,128]{3,2,1,0:T(8,128)(2,1)}), bf16[8,80,32,128]{3,2,1,0:T(8,128)(2,1)}, u32[]{:S(2)}, u32[]{:S(2)}) %all-to-all-start.3) | async-done | bytes 5242912 | tf_op jit(solution)/shard_map/all_to_all | solution.py:169
  499.2 5.7 %gather_fusion.3 = bf16[512,32,128]{2,1,0:T(8,128)(2,1)} fusion(bf16[640,32,128]{2,1,0:T(8,128)(2,1)} %bitcast.17, s32[1024]{0:T(1024)S(1)} %pad_clamp_fusion), kind=kCustom, calls=%fused_computation.3 | custom fusion | bytes 8390656 | tf_op jit(solution)/shard_map/jit(_take)/gather | solution.py:42
  504.9 6.8 %convert.1 = f32[2,256,32,128]{3,2,1,0:T(8,128)} convert(bf16[2,256,32,128]{3,2,1,0:T(8,128)(2,1)} %bitcast.56) | non-fusion elementwise | flops 2097152 | bytes 12582912 | tf_op jit(solution)/shard_map/convert_element_type | solution.py:170
  (30 shorter events, 0.3 us)
Async XLA Ops:
  7.2 8.0 %copy-start.2 = (s32[2048]{0:T(1024)S(1)}, s32[2048]{0:T(1024)}, u32[]{:S(2)}) copy-start(s32[2048]{0:T(1024)} %param.7) | copy-start | bytes 24580
  10.9 17.3 %all-to-all-start = ((bf16[4,32,1024]{2,1,0:T(8,128)(2,1)}), bf16[4,32,1024]{2,1,0:T(8,128)(2,1)S(1)}, u32[]{:S(2)}, u32[]{:S(2)}) async-start(bf16[4,32,1024]{2,1,0:T(8,128)(2,1)} %reshape.368), calls=%async_computation | async-start | bytes 524288 | tf_op jit(solution)/shard_map/all_to_all | solution.py:137
  28.1 148.2 %all-to-all-start.1 = ((bf16[8,80,32,128]{3,2,1,0:T(8,128)(2,1)}), bf16[8,80,32,128]{3,2,1,0:T(8,128)(2,1)}, u32[]{:S(2)}, u32[]{:S(2)}) async-start(bf16[8,80,32,128]{3,2,1,0:T(8,128)(2,1)} %bitcast.54), calls=%async_computation.1 | async-start | bytes 10485760 | tf_op jit(solution)/shard_map/all_to_all | solution.py:148
  34.7 123.4 %all-gather.3.cloned.1.call-start = ((), (), s32[]{:S(2)}) async-start(), calls=%async_computation.6 | async-start | bytes 2359296 | tf_op jit(solution)/shard_map/all_gather | solution.py:138
  35.6 200.2 %reduce-scatter.3.cloned.1.call-start = ((), (), s32[]{:S(2)}) async-start(), calls=%async_computation.7 | async-start | bytes 5242880 | tf_op jit(solution)/shard_map/reduce_scatter | solution.py:152
  165.8 16.2 %copy-start = (bf16[128,8,4,256]{3,1,2,0:T(8,128)(2,1)}, bf16[128,8,4,256]{3,1,2,0:T(8,128)(2,1)S(1)}, u32[]{:S(2)}) copy-start(bf16[128,8,4,256]{3,1,2,0:T(8,128)(2,1)S(1)} %copy.34) | copy-start | bytes 6291460
  192.0 45.3 %copy-start.1 = (bf16[256,1024]{1,0:T(8,128)(2,1)S(1)}, bf16[256,1024]{1,0:T(8,128)(2,1)}, u32[]{:S(2)}) copy-start(bf16[256,1024]{1,0:T(8,128)(2,1)} %param.5) | copy-start | bytes 1572868
  192.0 82.6 %all-gather.5.cloned.1.call-start = ((), (), s32[]{:S(2)}) async-start(), calls=%async_computation.8 | async-start | bytes 5242880 | tf_op jit(solution)/shard_map/all_gather | solution.py:164
  240.0 129.6 %reduce-scatter.5.cloned.1.call-start = ((), (), s32[]{:S(2)}) async-start(), calls=%async_computation.9 | async-start | bytes 2359296 | tf_op jit(solution)/shard_map/reduce_scatter | solution.py:176
  378.9 120.2 %all-to-all-start.3 = ((bf16[8,80,32,128]{3,2,1,0:T(8,128)(2,1)}), bf16[8,80,32,128]{3,2,1,0:T(8,128)(2,1)}, u32[]{:S(2)}, u32[]{:S(2)}) async-start(bf16[8,80,32,128]{3,2,1,0:T(8,128)(2,1)} %bitcast.55), calls=%async_computation.5 | async-start | bytes 10485760 | tf_op jit(solution)/shard_map/all_to_all | solution.py:169
Sparse Core Ops, SparseCore 0:
  38.2 119.8 all-gather.2
  192.1 43.6 reduce-scatter.2
  240.1 34.4 all-gather.4
  301.1 68.3 reduce-scatter.4

commit v2 on v1

--- a/solution.py
+++ b/solution.py
@@ -137,21 +137,25 @@
     by_group = lax.all_to_all(by_band, "dp", split_axis=0, concat_axis=0, tiled=True)
     banded = lax.all_gather(by_group, "tp", axis=1, tiled=True).reshape(tokens, depth)
 
-    both = jnp.arange(2, dtype=jnp.int32)
-    send_ix = send_slots.reshape(tp_size, 1, list_len) + both[None, :, None] * owned_count
-    in_ix = (from_place // list_len * 2 + both[:, None]) * list_len + from_place % list_len
-    back_ix = return_ix.reshape(tp_size, 1, list_len) + both[None, :, None] * owned_count
-    out_ix = (my_key // list_len * 2 + both[:, None]) * list_len + my_key % list_len
-    travel = (tp_size, 2 * list_len, band, tile)
-    own_rows = lax.dynamic_slice_in_dim(weight_tiles, me_dp * band, band, 2)
-    outgoing = take_tiles(own_rows, send_ix).reshape(travel)
-    arrived = lax.all_to_all(outgoing, "tp", split_axis=0, concat_axis=0, tiled=True)
-    weights = take_tiles(arrived, in_ix).reshape(2 * cols_dev, depth, tile)
-
-    partial = project(banded, weights)
-    proj = lax.psum_scatter(partial, "dp", scatter_dimension=0, tiled=True).astype(jnp.float32)
-    gate_proj = proj[:, :cols]
-    up_proj = proj[:, cols:]
+    travel = (tp_size, list_len, band, tile)
+    own_rows = [
+        lax.dynamic_slice(
+            weight_tiles, (m, 0, me_dp * band, 0), (1, owned_count, band, tile)
+        )
+        for m in range(2)
+    ]
+    outgoing = [take_tiles(own_rows[m], send_slots).reshape(travel) for m in range(2)]
+    weights, proj = [], []
+    for m in range(2):
+        with jax.named_scope(f"send{m}"):
+            arrived = lax.all_to_all(outgoing[m], "tp", split_axis=0, concat_axis=0, tiled=True)
+        with jax.named_scope(f"proj{m}"):
+            weights.append(take_tiles(arrived, from_place).reshape(cols_dev, depth, tile))
+            partial = project(banded, weights[m])
+            proj.append(
+                lax.psum_scatter(partial, "dp", scatter_dimension=0, tiled=True).astype(jnp.float32)
+            )
+    gate_proj, up_proj = proj
     sigmoid_gate = jax.nn.sigmoid(gate_proj)
     act_gate = gate_proj * sigmoid_gate
     hidden = (act_gate * up_proj).astype(jnp.bfloat16)
@@ -160,22 +164,37 @@
         cot_full * up_proj * (sigmoid_gate * (1.0 + gate_proj * (1.0 - sigmoid_gate)))
     ).astype(jnp.bfloat16)
     grad_up = (cot_full * act_gate).astype(jnp.bfloat16)
-    grads = jnp.concatenate([grad_gate, grad_up], axis=1)
-    grads = lax.all_gather(grads, "dp", axis=0, tiled=True)
-
-    summed = outer(banded.T, grads, tile).reshape(2 * owned_count, band, tile)
-    back = take_tiles(summed, back_ix).reshape(travel)
-    back, grads = lax.optimization_barrier((back, grads))
-    returned = lax.all_to_all(back, "tp", split_axis=0, concat_axis=0, tiled=True)
-    result = take_tiles(returned, out_ix).astype(jnp.float32)
-    result = result.reshape(2, owned_count, band, tile)
-
-    grads = grads.reshape(tokens, 2 * cols_dev, tile)
-    term = jnp.einsum("nbj,bkj->nk", grads, weights, preferred_element_type=jnp.float32)
-    term = term.astype(jnp.bfloat16).reshape(dp_size, tp_size, rows, depth).transpose(1, 0, 2, 3)
+    grads = [lax.all_gather(g, "dp", axis=0, tiled=True) for g in (grad_gate, grad_up)]
+    banded_t = banded.T
+    back = []
+    for m in range(2):
+        with jax.named_scope(f"outer{m}"):
+            summed = outer(banded_t, grads[m], tile).reshape(owned_count, band, tile)
+            back.append(take_tiles(summed, return_ix).reshape(travel))
+    back[1], grads[0], grads[1] = lax.optimization_barrier((back[1], grads[0], grads[1]))
+    result = []
+    for m in range(2):
+        with jax.named_scope(f"back{m}"):
+            returned = lax.all_to_all(back[m], "tp", split_axis=0, concat_axis=0, tiled=True)
+        result.append(take_tiles(returned, my_key).reshape(owned_count, band, tile))
+    result = jnp.stack(result).astype(jnp.float32)
+
+    with jax.named_scope("term"):
+        term = sum(
+            jnp.einsum(
+                "nbj,bkj->nk",
+                grads[m].reshape(tokens, cols_dev, tile),
+                weights[m],
+                preferred_element_type=jnp.float32,
+            )
+            for m in range(2)
+        )
+        term = term.astype(jnp.bfloat16).reshape(dp_size, tp_size, rows, depth)
+        term = term.transpose(1, 0, 2, 3)
     d_band = lax.psum_scatter(term.reshape(-1, depth), "tp", scatter_dimension=0, tiled=True)
     d_band = d_band.reshape(dp_size, rows, depth)
-    d_rows = lax.all_to_all(d_band, "dp", split_axis=0, concat_axis=0, tiled=True)
+    d_all = lax.all_gather(d_band, "dp", axis=0, tiled=False)
+    d_rows = lax.dynamic_index_in_dim(d_all, me_dp, 1, keepdims=False)
     d_normed = d_rows.reshape(dp_size, rows, tile_rows, band).transpose(1, 2, 0, 3)
     return (hidden, d_normed.reshape(rows, width), result)
 

time: 519 us -> 450 us (0.87)
  waiting for transfers between devices: 389 us -> 313 us
  blocking collectives: 9.38 us -> 0 us
  starting transfers between devices: 15.7 us -> 24.7 us
  local copies, waits for them, and re-layouts: 50.3 us -> 56.1 us
    all_gather x1, waiting for transfers between devices: 122 us -> 0.02 us  [local(): lax.all_gather(by_group, 'tp', axis=1, tiled=True).reshape(tokens, depth)]
    all_to_all x2 -> x4, waiting for transfers between devices: 120 us -> 175 us  [the longest x2 117 us: local(): lax.all_to_all(outgoing[m], 'tp', split_axis=0, concat_axis=0, tiled=True)]
    reduce_scatter x1 -> x2, waiting for transfers between devices: 43.8 us -> 30.4 us  [local(): lax.psum_scatter(partial, 'dp', scatter_dimension=0, tiled=True)]
    all_to_all x1 -> x0, blocking collectives: 9.38 us -> none  [local(): lax.all_to_all(d_band, 'dp', split_axis=0, concat_axis=0, tiled=True)]
    all_to_all x2 -> x4, starting transfers between devices: 11.2 us -> 20.1 us  [the longest x2 10.1 us: local(): lax.all_to_all(outgoing[m], 'tp', split_axis=0, concat_axis=0, tiled=True)]
    all_gather x1 -> x3, waiting for transfers between devices: 34.3 us -> 38.4 us  [the longest x2 35.6 us: local(): lax.all_gather(g, 'dp', axis=0, tiled=True)]
    gather x4 -> x8, local copies, waits for them, and re-layouts: 25.1 us -> 27.9 us  [take_tiles(): return jnp.take(flat, indices.reshape(-1), axis=0, mode='clip')]
    pallas_call x1 -> x2, Pallas kernels: 9.98 us -> 12.1 us  [outer(): pl.pallas_call(outer_kernel, grid=(blocks // 2, tokens // chunk), in_spec...]
  transfers between devices with their start and end apart: 7 -> 12, of which waited for: 6 -> 8; matrix products, arithmetic and copies ran while one was open for 5% -> 14% of each run, Pallas kernels for 0% -> 5%
where the time goes in v2:
time: 450 us; the launch traced here: 449 us
  waiting for transfers between devices  313 us (70%)
  local copies, waits for them, and re-layouts  56.1 us (12%)
  starting transfers between devices  24.7 us (5%)
  Pallas kernels  24.1 us (5%)
  between operations  14.3 us (3%)
  other arithmetic  9.59 us (2%)
  matrix products  7.27 us (2%)
    all_to_all x2, waiting for transfers between devices, local(): lax.all_to_all(outgoing[m], 'tp', split_axis=0, concat_axis=0, tiled=True)  117 us
    reduce_scatter x1, waiting for transfers between devices, local(): lax.psum_scatter(term.reshape(-1, depth), 'tp', scatter_dimension=0, tile...  68.5 us
    all_to_all x2, waiting for transfers between devices, local(): lax.all_to_all(back[m], 'tp', split_axis=0, concat_axis=0, tiled=True)  57.6 us
    all_gather x2, waiting for transfers between devices, local(): lax.all_gather(g, 'dp', axis=0, tiled=True)  35.6 us
    reduce_scatter x2, waiting for transfers between devices, local(): lax.psum_scatter(partial, 'dp', scatter_dimension=0, tiled=True)  30.4 us
    gather x8, local copies, waits for them, and re-layouts, take_tiles(): return jnp.take(flat, indices.reshape(-1), axis=0, mode='clip')  27.9 us
    pallas_call x2, Pallas kernels, outer(): pl.pallas_call(outer_kernel, grid=(blocks // 2, tokens // chunk), in_spec...  12.1 us
    pallas_call x2, Pallas kernels, project(): pl.pallas_call(project_kernel, grid=(tokens // chunk, blocks // 2), in_sp...  12 us
  transfers between devices with their start and end apart: 12, of which 8 were waited for; matrix products, arithmetic and copies ran while one was open for 14% of the time, Pallas kernels for 5%

profile of v2, /device:TPU:0, one launch (start us, length us, event | category | flops | bytes accessed | tf_op | source)
XLA Modules:
  0.0 449.1 jit_solution(13937275515895610190)
XLA Ops:
  7.2 1.7 reshape.247
  8.9 0.2 copy.60
  9.1 1.8 reshape.248
  10.9 4.2 all-to-all-start
  15.5 0.2 select_reduce_fusion.2
  15.7 4.3 dynamic-slice_bitcast_fusion.1
  20.0 4.1 gather_fusion
  24.2 6.5 %all-to-all-start.1 = ((bf16[8,40,32,128]{3,2,1,0:T(8,128)(2,1)}), bf16[8,40,32,128]{3,2,1,0:T(8,128)(2,1)}, u32[]{:S(2)}, u32[]{:S(2)}) async-start(bf16[8,40,32,128]{3,2,1,0:T(8,128)(2,1)} %bitcast.75), calls=%async_computation.1 | async-start | bytes 5242880 | tf_op jit(solution)/shard_map/send0/all_to_all | solution.py:151
  30.7 0.9 copy.38
  31.7 0.1 convolution_convert_fusion
  31.9 3.0 gather_fusion.2
  34.9 81.3 %all-to-all-done.1 = bf16[8,40,32,128]{3,2,1,0:T(8,128)(2,1)} async-done(((bf16[8,40,32,128]{3,2,1,0:T(8,128)(2,1)}), bf16[8,40,32,128]{3,2,1,0:T(8,128)(2,1)}, u32[]{:S(2)}, u32[]{:S(2)}) %all-to-all-start.1) | async-done | bytes 2621472 | tf_op jit(solution)/shard_map/send0/all_to_all | solution.py:151
  116.2 3.6 all-to-all-start.2
  119.9 0.3 select_reduce_fusion
  120.2 5.7 %copy.39 = bf16[4,256,1024]{1,0,2:T(4,128)(2,1)} copy(bf16[4,256,1024]{2,0,1:T(4,128)(2,1)} %all-gather.5.cloned.1.call-done) | data formatting | bytes 4194304 | tf_op jit(solution)/shard_map/all_gather | solution.py:138
  125.9 3.4 copy.49
  129.3 4.0 copy.40.banded_ref
  133.3 3.9 gather_fusion.1
  137.3 6.0 %proj0.1 = bf16[1024,1024]{1,0:T(8,128)(2,1)} custom-call(bf16[1024,1024]{1,0:T(8,128)(2,1)} %copy.40.banded_ref, bf16[8,1024,128]{2,1,0:T(8,128)(2,1)} %bitcast.89), custom_call_target="tpu_custom_call" | custom-call | flops 2147483648 | bytes 6291456 | tf_op jit(solution)/shard_map/proj0/pallas_call | solution.py:56
  143.4 36.1 %all-to-all-done.2 = bf16[8,40,32,128]{3,2,1,0:T(8,128)(2,1)S(1)} async-done(((bf16[8,40,32,128]{3,2,1,0:T(8,128)(2,1)}), bf16[8,40,32,128]{3,2,1,0:T(8,128)(2,1)S(1)}, u32[]{:S(2)}, u32[]{:S(2)}) %all-to-all-start.2) | async-done | bytes 2621472 | tf_op jit(solution)/shard_map/send1/all_to_all | solution.py:151
  179.5 2.2 gather_fusion.3
  181.7 6.0 %proj1.1 = bf16[1024,1024]{1,0:T(8,128)(2,1)} custom-call(bf16[1024,1024]{1,0:T(8,128)(2,1)} %copy.40.banded_ref, bf16[8,1024,128]{2,1,0:T(8,128)(2,1)} %bitcast.91), custom_call_target="tpu_custom_call" | custom-call | flops 2147483648 | bytes 6291456 | tf_op jit(solution)/shard_map/proj1/pallas_call | solution.py:56
  187.8 30.4 %reduce-scatter.6.cloned.1.call-done = bf16[256,1024]{1,0:T(8,128)(2,1)} async-done(((bf16[1024,1024]{1,0:T(8,128)(2,1)}), bf16[256,1024]{1,0:T(8,128)(2,1)}) %reduce-scatter.6.cloned.1.call-update) | async-done | bytes 524304 | tf_op jit(solution)/shard_map/proj1/reduce_scatter | solution.py:156
  218.2 3.0 fusion.9
  221.2 0.5 all-gather.9.cloned.1.call-update
  221.8 0.2 select_reduce_fusion.1
  222.1 21.9 %all-gather.7.cloned.1.call-done.grads_ref = bf16[1024,1024]{1,0:T(8,128)(2,1)} async-done(((bf16[256,1024]{1,0:T(8,128)(2,1)}), bf16[1024,1024]{1,0:T(8,128)(2,1)}) %all-gather.7.cloned.1.call-update) | async-done | bytes 2097168 | tf_op jit(solution)/shard_map/all_gather | solution.py:167
  243.9 6.0 %outer1.1 = bf16[8,1024,128]{2,1,0:T(8,128)(2,1)} custom-call(bf16[1024,1024]{1,0:T(8,128)(2,1)} %bitcast.79, bf16[1024,1024]{1,0:T(8,128)(2,1)} %all-gather.7.cloned.1.call-done.grads_ref), custom_call_target="tpu_custom_call" | custom-call | flops 2147483648 | bytes 6291456 | tf_op jit(solution)/shard_map/outer1/pallas_call | solution.py:97
  250.0 4.2 gather_fusion.4
  254.2 13.8 %all-gather.9.cloned.1.call-done.grads_ref = bf16[1024,1024]{1,0:T(8,128)(2,1)} async-done(((bf16[256,1024]{1,0:T(8,128)(2,1)}), bf16[1024,1024]{1,0:T(8,128)(2,1)}) %all-gather.9.cloned.1.call-update) | async-done | bytes 2097168 | tf_op jit(solution)/shard_map/all_gather | solution.py:167
  267.9 5.5 %all-to-all-start.4 = ((bf16[8,40,32,128]{3,2,1,0:T(8,128)(2,1)}), bf16[8,40,32,128]{3,2,1,0:T(8,128)(2,1)S(1)}, u32[]{:S(2)}, u32[]{:S(2)}) async-start(bf16[8,40,32,128]{3,2,1,0:T(8,128)(2,1)} %bitcast.14), calls=%async_computation.7 | async-start | bytes 5242880 | tf_op jit(solution)/shard_map/back1/all_to_all | solution.py:178
  273.5 0.2 reduce-scatter.8.cloned.1.call-start
  273.7 4.7 %fusion.3 = f32[1024,1024,1]{1,0,2:T(8,128)S(1)} fusion(bf16[8,1024,128]{2,1,0:T(8,128)(2,1)} %bitcast.90, bf16[1024,1024]{1,0:T(8,128)(2,1)} %all-gather.9.cloned.1.call-done.grads_ref), kind=kOutput, calls=%fused_computation.13 | convolution fusion | flops 2147483648 | bytes 8388608 | tf_op jit(solution)/shard_map/term/nbj,bkj->nk/dot_general | solution.py:184
  278.5 2.4 fusion
  280.9 1.6 copy.44
  282.4 6.0 %outer0.1 = bf16[8,1024,128]{2,1,0:T(8,128)(2,1)} custom-call(bf16[1024,1024]{1,0:T(8,128)(2,1)} %bitcast.80, bf16[1024,1024]{1,0:T(8,128)(2,1)} %all-gather.9.cloned.1.call-done.grads_ref), custom_call_target="tpu_custom_call" | custom-call | flops 2147483648 | bytes 6291456 | tf_op jit(solution)/shard_map/outer0/pallas_call | solution.py:97
  288.5 4.2 gather_fusion.5
  292.7 57.6 %all-to-all-done.4 = bf16[8,40,32,128]{3,2,1,0:T(8,128)(2,1)S(1)} async-done(((bf16[8,40,32,128]{3,2,1,0:T(8,128)(2,1)}), bf16[8,40,32,128]{3,2,1,0:T(8,128)(2,1)S(1)}, u32[]{:S(2)}, u32[]{:S(2)}) %all-to-all-start.4) | async-done | bytes 2621472 | tf_op jit(solution)/shard_map/back1/all_to_all | solution.py:178
  350.2 4.4 all-to-all-start.3
  354.7 68.5 %reduce-scatter.8.cloned.1.call-done = bf16[128,1024]{1,0:T(8,128)(2,1)} async-done(((bf16[1024,1024]{1,0:T(8,128)(2,1)}), bf16[128,1024]{1,0:T(8,128)(2,1)}) %reduce-scatter.8.cloned.1.call-update) | async-done | bytes 262160 | tf_op jit(solution)/shard_map/reduce_scatter | solution.py:194
  423.3 2.2 gather_fusion.7
  425.5 4.1 gather_fusion.6
  429.6 5.5 %maximum_convert_fusion = f32[2,256,32,128]{3,2,1,0:T(8,128)} fusion(bf16[1,256,32,128]{3,2,1,0:T(8,128)(2,1)S(1)} %bitcast.82, bf16[1,256,32,128]{3,2,1,0:T(8,128)(2,1)} %bitcast.83), kind=kLoop, calls=%fused_computation.8 | loop fusion | flops 4194304 | bytes 12582912 | tf_op jit(solution)/shard_map/convert_element_type | solution.py:180
  435.1 2.7 all-gather.11.cloned.1.call-done
  437.9 1.0 constant_dynamic-slice_fusion
  438.8 0.8 reshape.265
  439.6 0.8 copy.46
  440.4 1.8 reshape.266
  (43 shorter events, 1.0 us)
Async XLA Ops:
  8.9 6.4 %copy-start.3 = (s32[2048]{0:T(1024)S(1)}, s32[2048]{0:T(1024)}, u32[]{:S(2)}) copy-start(s32[2048]{0:T(1024)} %param.7) | copy-start | bytes 24580
  10.9 13.3 %all-to-all-start = ((bf16[4,32,1024]{2,1,0:T(8,128)(2,1)}), bf16[4,32,1024]{2,1,0:T(8,128)(2,1)S(1)}, u32[]{:S(2)}, u32[]{:S(2)}) async-start(bf16[4,32,1024]{2,1,0:T(8,128)(2,1)} %reshape.248), calls=%async_computation | async-start | bytes 524288 | tf_op jit(solution)/shard_map/all_to_all | solution.py:137
  24.2 92.0 %all-to-all-start.1 = ((bf16[8,40,32,128]{3,2,1,0:T(8,128)(2,1)}), bf16[8,40,32,128]{3,2,1,0:T(8,128)(2,1)}, u32[]{:S(2)}, u32[]{:S(2)}) async-start(bf16[8,40,32,128]{3,2,1,0:T(8,128)(2,1)} %bitcast.75), calls=%async_computation.1 | async-start | bytes 5242880 | tf_op jit(solution)/shard_map/send0/all_to_all | solution.py:151
  30.7 89.5 %all-gather.5.cloned.1.call-start = ((), (), s32[]{:S(2)}) async-start(), calls=%async_computation.8 | async-start | bytes 2359296 | tf_op jit(solution)/shard_map/all_gather | solution.py:138
  116.2 63.3 %all-to-all-start.2 = ((bf16[8,40,32,128]{3,2,1,0:T(8,128)(2,1)}), bf16[8,40,32,128]{3,2,1,0:T(8,128)(2,1)S(1)}, u32[]{:S(2)}, u32[]{:S(2)}) async-start(bf16[8,40,32,128]{3,2,1,0:T(8,128)(2,1)} %bitcast.74), calls=%async_computation.3 | async-start | bytes 5242880 | tf_op jit(solution)/shard_map/send1/all_to_all | solution.py:151
  119.8 68.0 %reduce-scatter.4.cloned.1.call-start = ((), (), s32[]{:S(2)}) async-start(), calls=%async_computation.9 | async-start | bytes 2621440 | tf_op jit(solution)/shard_map/proj0/reduce_scatter | solution.py:156
  143.3 74.9 %reduce-scatter.6.cloned.1.call-start = ((), (), s32[]{:S(2)}) async-start(), calls=%async_computation.10 | async-start | bytes 2621440 | tf_op jit(solution)/shard_map/proj1/reduce_scatter | solution.py:156
  187.7 30.5 %copy-start.2 = (bf16[256,1024]{1,0:T(8,128)(2,1)S(1)}, bf16[256,1024]{1,0:T(8,128)(2,1)}, u32[]{:S(2)}) copy-start(bf16[256,1024]{1,0:T(8,128)(2,1)} %param.5) | copy-start | bytes 1572868
  187.7 56.2 %all-gather.7.cloned.1.call-start = ((), (), s32[]{:S(2)}) async-start(), calls=%async_computation.11 | async-start | bytes 2621440 | tf_op jit(solution)/shard_map/all_gather | solution.py:167
  221.2 46.8 %all-gather.9.cloned.1.call-start = ((), (), s32[]{:S(2)}) async-start(), calls=%async_computation.12 | async-start | bytes 2621440 | tf_op jit(solution)/shard_map/all_gather | solution.py:167
  267.9 82.3 %all-to-all-start.4 = ((bf16[8,40,32,128]{3,2,1,0:T(8,128)(2,1)}), bf16[8,40,32,128]{3,2,1,0:T(8,128)(2,1)S(1)}, u32[]{:S(2)}, u32[]{:S(2)}) async-start(bf16[8,40,32,128]{3,2,1,0:T(8,128)(2,1)} %bitcast.14), calls=%async_computation.7 | async-start | bytes 5242880 | tf_op jit(solution)/shard_map/back1/all_to_all | solution.py:178
  273.5 149.7 %reduce-scatter.8.cloned.1.call-start = ((), (), s32[]{:S(2)}) async-start(), calls=%async_computation.13 | async-start | bytes 2359296 | tf_op jit(solution)/shard_map/reduce_scatter | solution.py:194
  273.7 4.8 %copy-start.1 = (bf16[256,32,128]{2,1,0:T(8,128)(2,1)S(1)}, bf16[256,32,128]{2,1,0:T(8,128)(2,1)}, u32[]{:S(2)}) copy-start(bf16[256,32,128]{2,1,0:T(8,128)(2,1)} %gather_fusion.3) | copy-start | bytes 6291460
  273.7 4.8 %copy-start.4 = (bf16[1024,1024]{1,0:T(8,128)(2,1)S(1)}, bf16[1024,1024]{1,0:T(8,128)(2,1)}, u32[]{:S(2)}) copy-start(bf16[1024,1024]{1,0:T(8,128)(2,1)} %all-gather.7.cloned.1.call-done.grads_ref) | copy-start | bytes 6291460
  350.2 75.2 %all-to-all-start.3 = ((bf16[8,40,32,128]{3,2,1,0:T(8,128)(2,1)}), bf16[8,40,32,128]{3,2,1,0:T(8,128)(2,1)}, u32[]{:S(2)}, u32[]{:S(2)}) async-start(bf16[8,40,32,128]{3,2,1,0:T(8,128)(2,1)} %bitcast.24), calls=%async_computation.6 | async-start | bytes 5242880 | tf_op jit(solution)/shard_map/back0/all_to_all | solution.py:178
  354.6 83.2 %all-gather.11.cloned.1.call-start = ((), (), s32[]{:S(2)}) async-start(), calls=%async_computation.14 | async-start | bytes 1310720 | tf_op jit(solution)/shard_map/all_gather | solution.py:196
  425.4 4.1 copy-start
Sparse Core Ops, SparseCore 0:
  34.2 82.3 all-gather.4
  143.4 32.6 reduce-scatter.3
  187.8 30.3 reduce-scatter.5
  221.3 22.5 all-gather.6
  245.3 22.5 all-gather.8
  282.6 140.5 reduce-scatter.7
  424.8 13.0 all-gather.10
